TPU v7x, 32 devices: a whole 2x2x4 slice. The times are simulated.
32 devices in a mesh: qa: 16 (over z, x, core), qb: 2 (over y).
Axes of the slice: x: 2, y: 2, z: 4, core: 2. Of those that a mesh axis runs over, the one named last changes fastest.
Arguments:
- wave_parts: float32 [2, 256, 128, 128], P(None, ('qa', 'qb')), may hold values from -6 to 6
- level_table: float32 [256, 128, 128], P(('qa', 'qb')), may hold values from -2 to 2
- phase_angles: float32 [2, 128], replicated, may hold values from 0.3 to 1.2
Outputs:
- final_parts: float32 [2, 256, 128, 128], P(None, ('qa', 'qb'))
All inputs are finite; a program needn't handle non-finite values.
Results may differ from a plain program's by a relative error of at most 0.0003.
Values sent between devices are 32-bit elements; how exact they have to be, the bound alone decides.
A program may use at most 64 MiB of HBM per device.

v0:
```python
import jax
import jax.numpy as jnp
from jax import lax
from jax.sharding import PartitionSpec as P

LAYERS = 2


def count_bits(values, count):
    places = jnp.arange(count.bit_length() - 1, dtype=jnp.int32)
    return jnp.sum(values[..., None] >> places & 1, axis=-1)


def sign_table(count):
    rank = jnp.arange(count, dtype=jnp.int32)
    parity = count_bits(rank[:, None] & rank[None, :], count) % 2
    real_part = jnp.where(parity == 1, -1.0, 1.0).astype(jnp.float32) * count ** (-0.5)
    return real_part


def turn_dim(values, dim):
    real_part = sign_table(values.shape[dim])
    moved = jnp.tensordot(values, real_part, axes=([dim], [0]), precision=lax.Precision.HIGHEST)
    return jnp.moveaxis(moved, -1, dim)


def turn_phase(values, levels, angle):
    turn = angle * levels
    return jnp.stack(
        [
            values[0] * jnp.cos(turn) + values[1] * jnp.sin(turn),
            values[1] * jnp.cos(turn) - values[0] * jnp.sin(turn),
        ]
    )


def body(wave_parts, level_table, phase_angles):
    values = wave_parts
    for layer in range(LAYERS):
        values = turn_phase(values, level_table, phase_angles[layer])
        values = turn_dim(values, 3)
        values = turn_dim(values, 2)
        moved = lax.all_to_all(values, "qa", split_axis=2, concat_axis=1, tiled=True)
        moved = turn_dim(moved, 1)
        values = lax.all_to_all(moved, "qa", split_axis=1, concat_axis=2, tiled=True)
        moved = lax.all_to_all(values, "qb", split_axis=3, concat_axis=1, tiled=True)
        spread = moved.reshape(2, lax.axis_size("qb"), -1, moved.shape[2], moved.shape[3])
        moved = turn_dim(spread, 1).reshape(moved.shape)
        values = lax.all_to_all(moved, "qb", split_axis=1, concat_axis=3, tiled=True)
    return values


def solution(mesh):
    in_specs = (P(None, ("qa", "qb"), None, None), P(("qa", "qb"), None, None), P())
    out_specs = P(None, ("qa", "qb"), None, None)
    return jax.shard_map(body, mesh=mesh, in_specs=in_specs, out_specs=out_specs, check_vma=False)
```

profile of v0, /device:TPU:0, one launch (start us, length us, event | category | flops | bytes accessed | tf_op | source)
XLA Modules:
  0.0 216.1 jit_solution(5427155283323233087)
XLA Ops:
  0.0 0.7 copy-done.1
  0.8 3.1 %fusion.15 = (f32[1,8,128,128]{3,2,1,0:T(8,128)S(1)}, f32[1,8,128,128]{3,2,1,0:T(8,128)S(1)}) fusion(f32[2,8,128,128]{3,2,1,0:T(8,128)} %param.3, f32[8,128,128]{2,1,0:T(8,128)} %param.4, f32[128]{0:T(128)S(1)} %get-tuple-element.12), kind=kLoop, calls=%fused_computation.25 | loop fusion | flops 917504 | bytes 2621952 | tf_op jit(solution)/shard_map/stack | solution.py:29
  3.9 1.1 fusion
  5.0 1.0 convolution_bitcast_fusion.5
  6.0 0.5 copy.64
  6.5 31.9 %all_to_all.135 = f32[2,8,128,128]{3,1,0,2:T(8,128)S(1)} all-to-all(f32[2,8,128,128]{3,1,0,2:T(8,128)S(1)} %copy.64), channel_id=1, replica_groups=mesh['qa'=16,'qb'=2] {'qa'}, dimensions={2} | all-to-all | bytes 2097152 | tf_op jit(solution)/shard_map/all_to_all | solution.py:43
  38.3 0.3 copy.66
  38.7 1.8 convolution_bitcast_fusion.4
  40.5 0.5 copy.68
  41.0 29.5 %all_to_all.136 = f32[2,128,8,128]{3,2,0,1:T(8,128)S(1)} all-to-all(f32[2,128,8,128]{3,2,0,1:T(8,128)S(1)} %copy.68), channel_id=1, replica_groups=mesh['qa'=16,'qb'=2] {'qa'}, dimensions={1} | all-to-all | bytes 2097152 | tf_op jit(solution)/shard_map/all_to_all | solution.py:45
  70.6 0.5 copy.71
  71.1 17.5 %all_to_all.137 = f32[2,8,128,128]{2,1,0,3:T(8,128)S(1)} all-to-all(f32[2,8,128,128]{2,1,0,3:T(8,128)S(1)} %copy.71), channel_id=1, replica_groups=mesh['qa'=16,'qb'=2] {'qb'}, dimensions={3} | all-to-all | bytes 2097152 | tf_op jit(solution)/shard_map/all_to_all | solution.py:46
  88.6 4.0 %convolution_bitcast_fusion.1 = f32[2,2,8,128,64]{3,1,4,2,0:T(2,128)S(1)} fusion(f32[2,8,128,2,64]{2,1,0,4,3:T(8,128)S(1)} %bitcast.112), kind=kOutput, calls=%fused_computation.1 | convolution fusion | flops 6291524 | bytes 2097152 | tf_op jit(solution)/shard_map/dot_general | solution.py:23
  92.6 0.1 copy.107
  92.7 16.5 %all_to_all.138 = f32[2,16,128,64]{2,3,0,1:T(8,128)S(1)} all-to-all(f32[2,16,128,64]{2,3,0,1:T(8,128)S(1)} %bitcast.113), channel_id=1, replica_groups=mesh['qa'=16,'qb'=2] {'qb'}, dimensions={1} | all-to-all | bytes 2097152 | tf_op jit(solution)/shard_map/all_to_all | solution.py:49
  109.4 0.2 copy.80
  109.7 0.2 copy.78
  109.9 0.8 copy-done
  110.7 2.0 add_bitcast_fusion
  112.7 1.1 fusion.4
  113.9 1.0 convolution_bitcast_fusion.3
  114.8 0.5 copy.84
  115.3 28.4 %all_to_all.139 = f32[2,8,128,128]{3,1,0,2:T(8,128)S(1)} all-to-all(f32[2,8,128,128]{3,1,0,2:T(8,128)S(1)} %copy.84), channel_id=1, replica_groups=mesh['qa'=16,'qb'=2] {'qa'}, dimensions={2} | all-to-all | bytes 2097152 | tf_op jit(solution)/shard_map/all_to_all | solution.py:43
  143.7 0.3 copy.86
  144.1 1.8 convolution_bitcast_fusion.2
  145.9 0.5 copy.88
  146.4 29.5 %all_to_all.140 = f32[2,128,8,128]{3,2,0,1:T(8,128)S(1)} all-to-all(f32[2,128,8,128]{3,2,0,1:T(8,128)S(1)} %copy.88), channel_id=1, replica_groups=mesh['qa'=16,'qb'=2] {'qa'}, dimensions={1} | all-to-all | bytes 2097152 | tf_op jit(solution)/shard_map/all_to_all | solution.py:45
  176.0 0.5 copy.91
  176.5 17.5 %all_to_all.141 = f32[2,8,128,128]{2,1,0,3:T(8,128)S(1)} all-to-all(f32[2,8,128,128]{2,1,0,3:T(8,128)S(1)} %copy.91), channel_id=1, replica_groups=mesh['qa'=16,'qb'=2] {'qb'}, dimensions={3} | all-to-all | bytes 2097152 | tf_op jit(solution)/shard_map/all_to_all | solution.py:46
  194.0 4.0 %convolution_bitcast_fusion = f32[2,2,8,128,64]{3,1,4,2,0:T(2,128)S(1)} fusion(f32[2,8,128,2,64]{2,1,0,4,3:T(8,128)S(1)} %bitcast.117), kind=kOutput, calls=%fused_computation | convolution fusion | flops 6291524 | bytes 2097152 | tf_op jit(solution)/shard_map/dot_general | solution.py:23
  198.1 16.6 %all_to_all.142 = f32[2,16,128,64]{2,3,0,1:T(8,128)S(1)} all-to-all(f32[2,16,128,64]{2,3,0,1:T(8,128)S(1)} %bitcast.118), channel_id=1, replica_groups=mesh['qa'=16,'qb'=2] {'qb'}, dimensions={1} | all-to-all | bytes 2097152 | tf_op jit(solution)/shard_map/all_to_all | solution.py:49
  214.8 1.3 copy.98
  (14 shorter events, 0.7 us)
Async XLA Ops:
  0.0 0.7 copy-start.1
  109.7 1.0 copy-start
where the time goes:
time: 217 us; the launch traced here: 216 us
  blocking collectives  187 us (86%)
  matrix products  15.7 us (7%)
  local copies, waits for them, and re-layouts  7.69 us (4%)
  other arithmetic  5.19 us (2%)
    all_to_all x2, blocking collectives, body(): lax.all_to_all(values, 'qa', split_axis=2, concat_axis=1, tiled=True)  60.2 us
    all_to_all x2, blocking collectives, body(): lax.all_to_all(moved, 'qa', split_axis=1, concat_axis=2, tiled=True)  59 us
    all_to_all x2, blocking collectives, body(): lax.all_to_all(values, 'qb', split_axis=3, concat_axis=1, tiled=True)  34.9 us
    all_to_all x2, blocking collectives, body(): lax.all_to_all(moved, 'qb', split_axis=1, concat_axis=3, tiled=True)  33.1 us
    dot_general x8, matrix products, turn_dim(): jnp.tensordot(values, real_part, axes=([dim], [0]), precision=lax.Precisi...  15.7 us
    another operation x2, other arithmetic, turn_phase(): jnp.stack([values[0] * jnp.cos(turn) + values[1] * jnp.sin(turn), values[...  5.09 us

commit v1 on v0

v1 whole, which is shorter than its diff:
```python
import functools

import jax
import jax.numpy as jnp
import numpy as np
from jax import lax
from jax.experimental import pallas as pl
from jax.experimental.pallas import tpu as pltpu
from jax.sharding import PartitionSpec as P

MESH = pl.DeviceIdType.MESH
TURN_MOST = 2.5


def fit_even(function, degree):
    top = TURN_MOST**2
    nodes = (np.cos(np.pi * (np.arange(64) + 0.5) / 64) + 1) * top / 2
    fit = np.polynomial.chebyshev.Chebyshev.fit(nodes, function(np.sqrt(nodes)), degree, domain=[0, top])
    return [float(c) for c in fit.convert(kind=np.polynomial.Polynomial).coef]


COS = fit_even(np.cos, 6)
SIN = fit_even(lambda t: np.sin(t) / t, 5)


def horner(coefs, u):
    total = jnp.float32(coefs[-1])
    for c in coefs[-2::-1]:
        total = total * u + jnp.float32(c)
    return total


def cos_sin(turn):
    u = turn * turn
    return horner(COS, u), turn * horner(SIN, u)


def sign_table(count, power):
    rank = np.arange(count)
    parity = np.zeros((count, count), np.int64)
    both = rank[:, None] & rank[None, :]
    while both.any():
        parity ^= both & 1
        both >>= 1
    return jnp.asarray((1.0 - 2.0 * parity) * 2.0**-power, jnp.bfloat16)


def mix_lead(x):
    n = x.shape[0]
    half = 1
    while half < n:
        y = x.reshape((n // (2 * half), 2, half) + x.shape[1:])
        x = jnp.stack([y[:, 0] + y[:, 1], y[:, 0] - y[:, 1]], axis=1).reshape(x.shape)
        half *= 2
    return x


def halves(x):
    hi = x.astype(jnp.bfloat16)
    return hi, (x - hi.astype(jnp.float32)).astype(jnp.bfloat16)


def mix_rows(table, x):
    hi, lo = halves(x)
    return jnp.dot(table, hi, preferred_element_type=jnp.float32) + jnp.dot(table, lo, preferred_element_type=jnp.float32)


def mix_lanes(x, table):
    hi, lo = halves(x)
    return jnp.dot(hi, table, preferred_element_type=jnp.float32) + jnp.dot(lo, table, preferred_element_type=jnp.float32)


def kernel(
    na, nb, wave_hbm, level_hbm, angle_ref, row0, lane0, row1, lane1, out_ref,
    wave, level, send0, got0, send1, got1, levels, cosine, sine,
    load_sem, own_sem, ssem, rsem,
):
    n = na * nb
    _, blocks, rows, lanes = wave.shape
    piece = send0.shape[2]
    per = rows // piece
    qa, qb = lax.axis_index("qa"), lax.axis_index("qb")
    me = qa * nb + qb

    def peer(k):
        to_a = lax.rem(qa + k // nb, na)
        to_b = lax.rem(qb + lax.rem(k, nb), nb)
        return to_a, to_b, to_a * nb + to_b

    barrier = pltpu.get_barrier_semaphore()

    @pl.loop(1, n)
    def _(k):
        to_a, to_b, _ = peer(k)
        pl.semaphore_signal(barrier, inc=1, device_id=(to_a, to_b), device_id_type=MESH)

    load_wave = pltpu.make_async_copy(wave_hbm, wave, load_sem.at[0])
    load_level = pltpu.make_async_copy(level_hbm, level, load_sem.at[1])
    load_level.start()
    load_wave.start()
    pl.semaphore_wait(barrier, n - 1)

    def exchange(source, target, slot):
        own = pltpu.make_async_copy(source.at[me], target.at[me], own_sem.at[slot])
        own.start()

        @pl.loop(0, n - 1)
        def _(i):
            k = lax.rem(i + (n // 2), n - 1) + 1
            to_a, to_b, to = peer(k)
            pltpu.make_async_remote_copy(
                src_ref=source.at[to], dst_ref=target.at[me], send_sem=ssem.at[slot], recv_sem=rsem.at[slot],
                device_id=(to_a, to_b), device_id_type=MESH,
            ).start()

        return own

    def finish(own, source, target, slot, sent):
        if not sent:
            own.wait()
        rest = (source if sent else target).at[pl.ds(0, n - 1)]
        pltpu.make_async_copy(rest, rest, (ssem if sent else rsem).at[slot]).wait()

    load_level.wait()
    own_levels = exchange(level, levels, 0)
    load_wave.wait()

    first = angle_ref[0:1, :]

    @pl.loop(0, blocks)
    def _(b):
        held = level[pl.ds(b * per, per)].reshape(rows, lanes)
        c, s = cos_sin(first * held)
        x, y = wave[0, b], wave[1, b]
        both = jnp.concatenate([x * c + y * s, y * c - x * s], axis=1)
        both = mix_rows(row0[...], both)
        wave[0, b] = mix_lanes(both[:, :lanes], lane0[...])
        wave[1, b] = mix_lanes(both[:, lanes:], lane0[...])

    for part in range(2):

        @pl.loop(0, rows // 16)
        def _(j):
            mixed = mix_lead(wave[part, :, pl.ds(pl.multiple_of(j * 16, 16), 16), :])
            for b in range(blocks):
                scatter(send0, part, b, j, mixed[b], per, piece)

    own0 = exchange(send0, got0, 1)

    finish(own_levels, level, levels, 0, False)
    second = angle_ref[1:2, :]

    @pl.loop(0, n)
    def _(d):
        c, s = cos_sin(second * levels[d])
        cosine[d] = c
        sine[d] = s

    finish(own0, send0, got0, 1, False)
    step = min(8, piece)

    @pl.loop(0, piece // step)
    def _(j):
        part = pl.ds(pl.multiple_of(j * step, step), step)
        x, y = mix_lead(got0[:, 0, part, :]), mix_lead(got0[:, 1, part, :])
        c, s = cosine[:, part, :], sine[:, part, :]
        send1[:, 0, part, :] = mix_lead(x * c + y * s)
        send1[:, 1, part, :] = mix_lead(y * c - x * s)

    own1 = exchange(send1, got1, 2)
    finish(own_levels, levels, levels, 0, True)
    finish(own0, send0, got0, 1, True)
    finish(own1, send1, got1, 2, False)

    @pl.loop(0, blocks)
    def _(b):
        held = pl.ds(b * per, per)
        both = jnp.concatenate(
            [got1[held, 0].reshape(rows, lanes), got1[held, 1].reshape(rows, lanes)], axis=1
        )
        both = mix_rows(row1[...], both)
        wave[0, b] = mix_lanes(both[:, :lanes], lane1[...])
        wave[1, b] = mix_lanes(both[:, lanes:], lane1[...])

    for part in range(2):

        @pl.loop(0, rows // 16)
        def _(j):
            held = pl.ds(pl.multiple_of(j * 16, 16), 16)
            out_ref[part, :, held, :] = mix_lead(wave[part, :, held, :])

    finish(own1, send1, got1, 2, True)


def scatter(send, part, b, j, values, per, piece):
    if piece >= 16:
        steps = piece // 16
        send[b * per + j // steps, part, pl.ds(pl.multiple_of(lax.rem(j, steps) * 16, 16), 16), :] = values
    else:
        for i in range(16 // piece):
            send[b * per + j * (16 // piece) + i, part] = values[i * piece : (i + 1) * piece]


def body(wave_parts, level_table, phase_angles):
    na, nb = lax.axis_size("qa"), lax.axis_size("qb")
    n = na * nb
    _, blocks, rows, lanes = wave_parts.shape
    piece = blocks * rows // n
    bits = (n * blocks * rows * lanes).bit_length() - 1
    powers = [(bits + i) // 4 for i in range(4)]
    tables = [sign_table(rows if i % 2 == 0 else lanes, p) for i, p in enumerate(powers)]
    vmem = pl.BlockSpec(memory_space=pltpu.VMEM)
    hbm = pl.BlockSpec(memory_space=pl.ANY)
    f32 = jnp.float32
    state = pltpu.VMEM((n, 2, piece, lanes), f32)
    table = pltpu.VMEM((n, piece, lanes), f32)
    return pl.pallas_call(
        functools.partial(kernel, na, nb),
        out_shape=jax.ShapeDtypeStruct(wave_parts.shape, f32),
        in_specs=[hbm, hbm, vmem, vmem, vmem, vmem, vmem],
        out_specs=vmem,
        scratch_shapes=[
            pltpu.VMEM(wave_parts.shape, f32),
            table,
            state, state, state, state, table, table, table,
            pltpu.SemaphoreType.DMA((2,)),
            pltpu.SemaphoreType.DMA((3,)),
            pltpu.SemaphoreType.DMA((3,)),
            pltpu.SemaphoreType.DMA((3,)),
        ],
        compiler_params=pltpu.CompilerParams(
            collective_id=0, has_side_effects=True, vmem_limit_bytes=40 * 2**20
        ),
    )(wave_parts, level_table.reshape(n, piece, lanes), phase_angles, *tables)


def solution(mesh):
    in_specs = (P(None, ("qa", "qb"), None, None), P(("qa", "qb"), None, None), P())
    out_specs = P(None, ("qa", "qb"), None, None)
    return jax.shard_map(body, mesh=mesh, in_specs=in_specs, out_specs=out_specs, check_vma=False)
```

time: 217 us -> 75.9 us (0.35)
  blocking collectives: 187 us -> 0 us
  Pallas kernels: 0 us -> 69.4 us
  matrix products: 15.7 us -> 0 us
  other arithmetic: 5.19 us -> 0 us
  local copies, waits for them, and re-layouts: 7.69 us -> 5.43 us
    all_to_all x8 -> x0, blocking collectives: 187 us -> none  [the longest x2 60.2 us: body(): lax.all_to_all(values, 'qa', split_axis=2, concat_axis=1, tiled=True)]
    pallas_call x0 -> x1, Pallas kernels: none -> 69.4 us  [body(): pl.pallas_call(functools.partial(kernel, na, nb), out_shape=jax.ShapeDtyp...]
    dot_general x8 -> x0, matrix products: 15.7 us -> none  [turn_dim(): jnp.tensordot(values, real_part, axes=([dim], [0]), precision=lax.Precisi...]
    another operation x2 -> x0, other arithmetic: 5.09 us -> none  [turn_phase(): jnp.stack([values[0] * jnp.cos(turn) + values[1] * jnp.sin(turn), values[...]
    unnamed x4 -> x11, local copies, waits for them, and re-layouts: 1.5 us -> 5.43 us
    all_to_all x9 -> x0, local copies, waits for them, and re-layouts: 3.37 us -> none  [the longest x3 1.48 us: body(): lax.all_to_all(moved, 'qb', split_axis=1, concat_axis=3, tiled=True)]
where the time goes in v1:
time: 75.9 us; the launch traced here: 74.8 us
  Pallas kernels  69.4 us (91%)
  local copies, waits for them, and re-layouts  5.43 us (7%)
    pallas_call x1, Pallas kernels, body(): pl.pallas_call(functools.partial(kernel, na, nb), out_shape=jax.ShapeDtyp...  69.4 us
    unnamed x11, local copies, waits for them, and re-layouts  5.43 us

profile of v1, /device:TPU:0, one launch (start us, length us, event | category | flops | bytes accessed | tf_op | source)
XLA Modules:
  0.0 74.8 jit_solution(6322757496111537978)
XLA Ops:
  0.0 0.0 copy-start.4
  0.0 0.7 copy-done.4
  0.7 0.0 copy-start
  0.7 1.2 %copy-done = f32[2,8,128,128]{3,2,1,0:T(8,128)S(1)} copy-done((f32[2,8,128,128]{3,2,1,0:T(8,128)S(1)}, f32[2,8,128,128]{3,2,1,0:T(8,128)}, u32[]{:S(2)}) %copy-start) | copy-done | bytes 1048600
  1.9 0.0 copy-start.1
  1.9 1.0 %copy-done.1 = f32[8,128,128]{2,1,0:T(8,128)S(1)} copy-done((f32[8,128,128]{2,1,0:T(8,128)S(1)}, f32[8,128,128]{2,1,0:T(8,128)}, u32[]{:S(2)}) %copy-start.1) | copy-done | bytes 524312
  2.9 0.0 copy-start.2
  2.9 0.8 %copy-done.2 = bf16[128,128]{1,0:T(8,128)(2,1)S(1)} copy-done((bf16[128,128]{1,0:T(8,128)(2,1)S(1)}, bf16[128,128]{1,0:T(8,128)(2,1)}, u32[]{:S(2)}) %copy-start.2) | copy-done | bytes 32792
  3.7 0.0 copy-start.3
  3.7 0.8 %copy-done.3 = bf16[128,128]{1,0:T(8,128)(2,1)S(1)} copy-done((bf16[128,128]{1,0:T(8,128)(2,1)S(1)}, bf16[128,128]{1,0:T(8,128)(2,1)}, u32[]{:S(2)}) %copy-start.3) | copy-done | bytes 32792
  4.5 69.4 %shard_map.73 = f32[2,8,128,128]{3,2,1,0:T(8,128)S(1)} custom-call(f32[2,8,128,128]{3,2,1,0:T(8,128)S(1)} %copy-done, f32[32,32,128]{2,1,0:T(8,128)S(1)} %bitcast.1, f32[2,128]{1,0:T(2,128)S(1)} %copy-done.4, bf16[128,128]{1,0:T(8,128)(2,1)S(1)} %copy-done.3, bf16[128,128]{1,0:T(8,128)(2,1)S(1)} %copy-done.3, bf16[128,128]{1,0:T(8,128)(2,1)S(1)} %copy-done.2, ...), custom_call_target="tpu_custom_call" | custom-call | tf_op jit(solution)/shard_map/pallas_call | solution.py:217
  73.9 1.0 %copy.9 = f32[2,8,128,128]{3,2,1,0:T(8,128)} copy(f32[2,8,128,128]{3,2,1,0:T(8,128)S(1)} %shard_map.73) | data formatting | bytes 2097152
Async XLA Ops:
  0.0 0.7 copy-start.4
  0.7 1.2 %copy-start = (f32[2,8,128,128]{3,2,1,0:T(8,128)S(1)}, f32[2,8,128,128]{3,2,1,0:T(8,128)}, u32[]{:S(2)}) copy-start(f32[2,8,128,128]{3,2,1,0:T(8,128)} %wave_hbm.1) | copy-start | bytes 3145732
  1.9 1.0 %copy-start.1 = (f32[8,128,128]{2,1,0:T(8,128)S(1)}, f32[8,128,128]{2,1,0:T(8,128)}, u32[]{:S(2)}) copy-start(f32[8,128,128]{2,1,0:T(8,128)} %param.8) | copy-start | bytes 1572868
  2.9 0.8 %copy-start.2 = (bf16[128,128]{1,0:T(8,128)(2,1)S(1)}, bf16[128,128]{1,0:T(8,128)(2,1)}, u32[]{:S(2)}) copy-start(bf16[128,128]{1,0:T(8,128)(2,1)} %constant.5.clone.row1.lane1) | copy-start | bytes 98308
  3.7 0.8 %copy-start.3 = (bf16[128,128]{1,0:T(8,128)(2,1)S(1)}, bf16[128,128]{1,0:T(8,128)(2,1)}, u32[]{:S(2)}) copy-start(bf16[128,128]{1,0:T(8,128)(2,1)} %constant.4.clone.row0.lane0) | copy-start | bytes 98308

commit v2 on v0

v2 whole, which is shorter than its diff:
```python
import functools

import jax
import jax.numpy as jnp
import numpy as np
from jax import lax
from jax.experimental import pallas as pl
from jax.experimental.pallas import tpu as pltpu
from jax.sharding import PartitionSpec as P

MESH = pl.DeviceIdType.MESH
TURN_MOST = 2.5


def fit_even(function, degree):
    top = TURN_MOST**2
    nodes = (np.cos(np.pi * (np.arange(64) + 0.5) / 64) + 1) * top / 2
    fit = np.polynomial.chebyshev.Chebyshev.fit(nodes, function(np.sqrt(nodes)), degree, domain=[0, top])
    return [float(c) for c in fit.convert(kind=np.polynomial.Polynomial).coef]


COS = fit_even(np.cos, 6)
SIN = fit_even(lambda t: np.sin(t) / t, 5)


def horner(coefs, u, scale):
    total = jnp.float32(coefs[-1] * scale)
    for c in coefs[-2::-1]:
        total = total * u + jnp.float32(c * scale)
    return total


def cos_sin(turn, scale):
    u = turn * turn
    return horner(COS, u, scale), turn * horner(SIN, u, scale)


def sign_table(count):
    both = lax.broadcasted_iota(jnp.int32, (count, count), 0) & lax.broadcasted_iota(jnp.int32, (count, count), 1)
    shift = 1
    while shift < count.bit_length():
        shift *= 2
    while shift > 1:
        shift //= 2
        both = both ^ (both >> shift)
    return (1 - 2 * (both & 1)).astype(jnp.float32).astype(jnp.bfloat16)


def mix_lead(x):
    n = x.shape[0]
    half = 1
    while half < n:
        y = x.reshape((n // (2 * half), 2, half) + x.shape[1:])
        x = jnp.stack([y[:, 0] + y[:, 1], y[:, 0] - y[:, 1]], axis=1).reshape(x.shape)
        half *= 2
    return x


def dot(a, b):
    return jnp.dot(a, b, preferred_element_type=jnp.float32)


def halves(x):
    hi = x.astype(jnp.bfloat16)
    return hi, (x - hi.astype(jnp.float32)).astype(jnp.bfloat16)


def mix_rows_lanes(rows, lanes, x, y):
    hi, lo = halves(jnp.concatenate([x, y], axis=1))
    both = dot(rows, hi) + dot(rows, lo)
    width = x.shape[1]
    out = []
    for part in (both[:, :width], both[:, width:]):
        hi, lo = halves(part)
        out.append(dot(hi, lanes) + dot(lo, lanes))
    return out


def kernel(
    na, nb, scales, wave_hbm, level_hbm, angle_hbm, out_ref,
    wave, level, angle, rows_table, lanes_table, mixed, send0, got0, send1, got1, levels, cosine, sine,
    load_sem, own_sem, ssem, rsem, level_sem,
):
    n = na * nb
    cuts, _, _, step, lanes = send0.shape
    qa, qb = lax.axis_index("qa"), lax.axis_index("qb")
    me = qa * nb + qb

    def flips(q, count):
        found = [q]
        bit = 1
        while bit < count:
            change = bit - 2 * bit * lax.rem(q // bit, 2)
            found = found + [f + change for f in found]
            bit *= 2
        return found

    to_as, to_bs = flips(qa, na), flips(qb, nb)
    order = [(ka, kb) for ka in far_first(na) for kb in range(nb - 1, -1, -1) if ka or kb]
    peers = [(to_as[ka], to_bs[kb], to_as[ka] * nb + to_bs[kb]) for ka, kb in order]

    load_wave = pltpu.make_async_copy(wave_hbm, wave, load_sem.at[0])
    load_level = pltpu.make_async_copy(level_hbm, level, load_sem.at[1])
    load_angle = pltpu.make_async_copy(angle_hbm, angle, load_sem.at[2])
    load_level.start()
    load_angle.start()
    load_wave.start()

    barrier = pltpu.get_barrier_semaphore()
    for to_a, to_b, _ in peers:
        pl.semaphore_signal(barrier, inc=1, device_id=(to_a, to_b), device_id_type=MESH)

    rows_table[...] = sign_table(n * step)
    lanes_table[...] = sign_table(lanes)
    load_level.wait()
    pl.semaphore_wait(barrier, n - 1)

    def exchange(source, target, own, sent, got):
        pltpu.make_async_copy(source.at[me], target.at[me], own).start()
        for to_a, to_b, to in peers:
            pltpu.make_async_remote_copy(
                src_ref=source.at[to], dst_ref=target.at[me], send_sem=sent, recv_sem=got,
                device_id=(to_a, to_b), device_id_type=MESH,
            ).start()

    def received(source, target, own, got):
        pltpu.make_async_copy(source.at[me], target.at[me], own).wait()
        rest = target.at[pl.ds(0, n - 1)]
        pltpu.make_async_copy(rest, rest, got).wait()

    def left(source, sent):
        rest = source.at[pl.ds(0, n - 1)]
        pltpu.make_async_copy(rest, rest, sent).wait()

    exchange(level, levels, level_sem.at[0], level_sem.at[1], level_sem.at[2])
    load_angle.wait()
    load_wave.wait()

    first = angle[0:1, :]

    @pl.loop(0, cuts)
    def _(cut):
        held = pl.ds(pl.multiple_of(cut * step, step), step)
        c, s = cos_sin(first * level[:, held, :].reshape(n * step, lanes), scales[0])
        x = wave[0, :, held, :].reshape(n * step, lanes)
        y = wave[1, :, held, :].reshape(n * step, lanes)
        done = mix_rows_lanes(rows_table[...], lanes_table[...], x * c + y * s, y * c - x * s)
        for part in range(2):
            mixed[cut, part] = done[part].reshape(n, step, lanes)

    group = 4
    for part in range(2):

        @pl.loop(0, n // group)
        def _(i):
            ds = pl.ds(i * group, group)
            send0[:, ds, part] = mix_lead(mixed[:, part, ds])

    @pl.loop(0, cuts)
    def _(cut):
        exchange(send0.at[cut], got0.at[cut], own_sem.at[0, cut], ssem.at[0, cut], rsem.at[0, cut])

    received(level, levels, level_sem.at[0], level_sem.at[2])
    second = angle[1:2, :]

    @pl.loop(0, n)
    def _(d):
        c, s = cos_sin(second * levels[d], scales[1])
        cosine[d] = c
        sine[d] = s

    @pl.loop(0, cuts)
    def _(cut):
        received(send0.at[cut], got0.at[cut], own_sem.at[0, cut], rsem.at[0, cut])
        held = pl.ds(pl.multiple_of(cut * step, step), step)
        x, y = mix_lead(got0[cut, :, 0]), mix_lead(got0[cut, :, 1])
        c, s = cosine[:, held, :], sine[:, held, :]
        send1[cut, :, 0] = mix_lead(x * c + y * s)
        send1[cut, :, 1] = mix_lead(y * c - x * s)
        exchange(send1.at[cut], got1.at[cut], own_sem.at[1, cut], ssem.at[1, cut], rsem.at[1, cut])

    @pl.loop(0, cuts)
    def _(cut):
        received(send1.at[cut], got1.at[cut], own_sem.at[1, cut], rsem.at[1, cut])
        x, y = (got1[cut, :, part].reshape(n * step, lanes) for part in range(2))
        done = mix_rows_lanes(rows_table[...], lanes_table[...], x, y)
        for part in range(2):
            mixed[cut, part] = done[part].reshape(n, step, lanes)

    for part in range(2):

        @pl.loop(0, n // group)
        def _(i):
            ds = pl.ds(i * group, group)
            done = mix_lead(mixed[:, part, ds])
            for cut in range(cuts):
                out_ref[part, ds, cut * step : (cut + 1) * step, :] = done[cut]

    left(level, level_sem.at[1])

    @pl.loop(0, cuts)
    def _(cut):
        left(send0.at[cut], ssem.at[0, cut])
        left(send1.at[cut], ssem.at[1, cut])


def far_first(count):
    return range(count - 1, -1, -1)


STEP = 8


def body(wave_parts, level_table, phase_angles):
    na, nb = lax.axis_size("qa"), lax.axis_size("qb")
    n = na * nb
    _, blocks, rows, lanes = wave_parts.shape
    piece = blocks * rows // n
    step = min(STEP, piece)
    cuts = piece // step
    bits = (n * blocks * rows * lanes).bit_length() - 1
    scales = (2.0 ** -(bits // 2), 2.0 ** -(bits - bits // 2))
    hbm = pl.BlockSpec(memory_space=pl.ANY)
    f32 = jnp.float32
    flat = (2, n, piece, lanes)
    state = pltpu.VMEM((cuts, n, 2, step, lanes), f32)
    table = pltpu.VMEM((n, piece, lanes), f32)
    result = pl.pallas_call(
        functools.partial(kernel, na, nb, scales),
        out_shape=jax.ShapeDtypeStruct(flat, f32),
        in_specs=[hbm, hbm, hbm],
        out_specs=pl.BlockSpec(memory_space=pltpu.VMEM),
        scratch_shapes=[
            pltpu.VMEM(flat, f32),
            table,
            pltpu.VMEM(phase_angles.shape, f32),
            pltpu.VMEM((n * step, n * step), jnp.bfloat16),
            pltpu.VMEM((lanes, lanes), jnp.bfloat16),
            pltpu.VMEM((cuts, 2, n, step, lanes), f32),
            state, state, state, state, table, table, table,
            pltpu.SemaphoreType.DMA((3,)),
            pltpu.SemaphoreType.DMA((2, cuts)),
            pltpu.SemaphoreType.DMA((2, cuts)),
            pltpu.SemaphoreType.DMA((2, cuts)),
            pltpu.SemaphoreType.DMA((3,)),
        ],
        compiler_params=pltpu.CompilerParams(
            collective_id=0, has_side_effects=True, vmem_limit_bytes=50 * 2**20
        ),
    )(wave_parts.reshape(flat), level_table.reshape(n, piece, lanes), phase_angles)
    return result.reshape(wave_parts.shape)


def solution(mesh):
    in_specs = (P(None, ("qa", "qb"), None, None), P(("qa", "qb"), None, None), P())
    out_specs = P(None, ("qa", "qb"), None, None)
    return jax.shard_map(body, mesh=mesh, in_specs=in_specs, out_specs=out_specs, check_vma=False)
```

time: 217 us -> 70.1 us (0.32)
  blocking collectives: 187 us -> 0 us
  Pallas kernels: 0 us -> 65.9 us
  matrix products: 15.7 us -> 0 us
  other arithmetic: 5.19 us -> 0 us
  local copies, waits for them, and re-layouts: 7.69 us -> 3.92 us
    all_to_all x8 -> x0, blocking collectives: 187 us -> none  [the longest x2 60.2 us: body(): lax.all_to_all(values, 'qa', split_axis=2, concat_axis=1, tiled=True)]
    pallas_call x0 -> x1, Pallas kernels: none -> 65.9 us  [body(): pl.pallas_call(functools.partial(kernel, na, nb, scales), out_shape=jax.S...]
    dot_general x8 -> x0, matrix products: 15.7 us -> none  [turn_dim(): jnp.tensordot(values, real_part, axes=([dim], [0]), precision=lax.Precisi...]
    another operation x2 -> x0, other arithmetic: 5.09 us -> none  [turn_phase(): jnp.stack([values[0] * jnp.cos(turn) + values[1] * jnp.sin(turn), values[...]
    all_to_all x9 -> x0, local copies, waits for them, and re-layouts: 3.37 us -> none  [the longest x3 1.48 us: body(): lax.all_to_all(moved, 'qb', split_axis=1, concat_axis=3, tiled=True)]
    unnamed x4 -> x7, local copies, waits for them, and re-layouts: 1.5 us -> 3.92 us
where the time goes in v2:
time: 70.1 us; the launch traced here: 69.9 us
  Pallas kernels  65.9 us (94%)
  local copies, waits for them, and re-layouts  3.92 us (6%)
    pallas_call x1, Pallas kernels, body(): pl.pallas_call(functools.partial(kernel, na, nb, scales), out_shape=jax.S...  65.9 us
    unnamed x7, local copies, waits for them, and re-layouts  3.92 us

profile of v2, /device:TPU:0, one launch (start us, length us, event | category | flops | bytes accessed | tf_op | source)
XLA Modules:
  0.0 69.9 jit_solution(15167471339225017676)
XLA Ops:
  0.0 0.0 copy-start.2
  0.0 0.7 copy-done.2
  0.7 0.0 copy-start
  0.7 1.2 %copy-done = f32[2,8,128,128]{3,2,1,0:T(8,128)S(1)} copy-done((f32[2,8,128,128]{3,2,1,0:T(8,128)S(1)}, f32[2,8,128,128]{3,2,1,0:T(8,128)}, u32[]{:S(2)}) %copy-start) | copy-done | bytes 1048600
  1.9 0.0 copy-start.1
  1.9 1.0 %copy-done.1 = f32[8,128,128]{2,1,0:T(8,128)S(1)} copy-done((f32[8,128,128]{2,1,0:T(8,128)S(1)}, f32[8,128,128]{2,1,0:T(8,128)}, u32[]{:S(2)}) %copy-start.1) | copy-done | bytes 524312
  2.9 65.9 %shard_map.37 = f32[2,32,32,128]{3,2,1,0:T(8,128)S(1)} custom-call(f32[2,32,32,128]{3,2,1,0:T(8,128)S(1)} %bitcast.4, f32[32,32,128]{2,1,0:T(8,128)S(1)} %bitcast.5, f32[2,128]{1,0:T(2,128)S(1)} %copy-done.2), custom_call_target="tpu_custom_call" | custom-call | tf_op jit(solution)/shard_map/pallas_call | solution.py:228
  68.9 1.0 %copy.5 = f32[2,8,128,128]{3,2,1,0:T(8,128)} copy(f32[2,8,128,128]{3,2,1,0:T(8,128)S(1)} %bitcast.3) | data formatting | bytes 2097152
Async XLA Ops:
  0.0 0.7 copy-start.2
  0.7 1.2 %copy-start = (f32[2,8,128,128]{3,2,1,0:T(8,128)S(1)}, f32[2,8,128,128]{3,2,1,0:T(8,128)}, u32[]{:S(2)}) copy-start(f32[2,8,128,128]{3,2,1,0:T(8,128)} %param.3) | copy-start | bytes 3145732
  1.9 1.0 %copy-start.1 = (f32[8,128,128]{2,1,0:T(8,128)S(1)}, f32[8,128,128]{2,1,0:T(8,128)}, u32[]{:S(2)}) copy-start(f32[8,128,128]{2,1,0:T(8,128)} %param.4) | copy-start | bytes 1572868

commit v3 on v2

--- a/solution.py
+++ b/solution.py
@@ -85,6 +85,7 @@
     cuts, _, _, step, lanes = send0.shape
     qa, qb = lax.axis_index("qa"), lax.axis_index("qb")
     me = qa * nb + qb
+    group = 4
 
     def flips(q, count):
         found = [q]
@@ -96,7 +97,7 @@
         return found
 
     to_as, to_bs = flips(qa, na), flips(qb, nb)
-    order = [(ka, kb) for ka in far_first(na) for kb in range(nb - 1, -1, -1) if ka or kb]
+    order = [(ka, kb) for ka in far_first(na) for kb in range(nb) if ka or kb]
     peers = [(to_as[ka], to_bs[kb], to_as[ka] * nb + to_bs[kb]) for ka, kb in order]
 
     load_wave = pltpu.make_async_copy(wave_hbm, wave, load_sem.at[0])
@@ -107,11 +108,9 @@
     load_wave.start()
 
     barrier = pltpu.get_barrier_semaphore()
-    for to_a, to_b, _ in peers:
+    for to_a, to_b, _ in peers[::-1]:
         pl.semaphore_signal(barrier, inc=1, device_id=(to_a, to_b), device_id_type=MESH)
 
-    rows_table[...] = sign_table(n * step)
-    lanes_table[...] = sign_table(lanes)
     load_level.wait()
     pl.semaphore_wait(barrier, n - 1)
 
@@ -133,6 +132,8 @@
         pltpu.make_async_copy(rest, rest, sent).wait()
 
     exchange(level, levels, level_sem.at[0], level_sem.at[1], level_sem.at[2])
+    rows_table[...] = sign_table(n * step)
+    lanes_table[...] = sign_table(lanes)
     load_angle.wait()
     load_wave.wait()
 
@@ -148,7 +149,6 @@
         for part in range(2):
             mixed[cut, part] = done[part].reshape(n, step, lanes)
 
-    group = 4
     for part in range(2):
 
         @pl.loop(0, n // group)
@@ -205,7 +205,9 @@
 
 
 def far_first(count):
-    return range(count - 1, -1, -1)
+    quarter = count // 4
+    low = [*range(0, quarter, 2), *range(1, quarter, 2)]
+    return [high * quarter + k for high in (2, 3, 1, 0) for k in low] if quarter else range(count - 1, -1, -1)
 
 
 STEP = 8
@@ -245,7 +247,7 @@
             pltpu.SemaphoreType.DMA((3,)),
         ],
         compiler_params=pltpu.CompilerParams(
-            collective_id=0, has_side_effects=True, vmem_limit_bytes=50 * 2**20
+            collective_id=0, has_side_effects=True, vmem_limit_bytes=62 * 2**20
         ),
     )(wave_parts.reshape(flat), level_table.reshape(n, piece, lanes), phase_angles)
     return result.reshape(wave_parts.shape)

time: 70.1 us -> 67.6 us (0.964)
  local copies, waits for them, and re-layouts: 3.92 us -> 2.3 us
  Pallas kernels: 65.9 us -> 65.1 us
    unnamed x7 -> x1, local copies, waits for them, and re-layouts: 3.92 us -> 2.3 us
    pallas_call x1, Pallas kernels: 65.9 us -> 65.1 us  [body(): pl.pallas_call(functools.partial(kernel, na, nb, scales), out_shape=jax.S...]
where the time goes in v3:
time: 67.6 us; the launch traced here: 67.4 us
  Pallas kernels  65.1 us (96%)
  local copies, waits for them, and re-layouts  2.3 us (3%)
    pallas_call x1, Pallas kernels, body(): pl.pallas_call(functools.partial(kernel, na, nb, scales), out_shape=jax.S...  65.1 us
    unnamed x1, local copies, waits for them, and re-layouts  2.3 us

profile of v3, /device:TPU:0, one launch (start us, length us, event | category | flops | bytes accessed | tf_op | source)
XLA Modules:
  0.0 67.4 jit_solution(16729475831503557768)
XLA Ops:
  0.0 65.1 %shard_map.37 = f32[2,32,32,128]{3,2,1,0:T(8,128)} custom-call(f32[2,32,32,128]{3,2,1,0:T(8,128)} %bitcast.4, f32[32,32,128]{2,1,0:T(8,128)} %bitcast.5, f32[2,128]{1,0:T(2,128)} %angle_hbm.1), custom_call_target="tpu_custom_call" | custom-call | tf_op jit(solution)/shard_map/pallas_call | solution.py:230
  65.1 2.3 %copy.5 = f32[2,8,128,128]{3,2,1,0:T(8,128)} copy(f32[2,8,128,128]{3,2,1,0:T(8,128)} %bitcast.3) | data formatting | bytes 2097152

commit v4 on v3

--- a/solution.py
+++ b/solution.py
@@ -210,7 +210,7 @@
     return [high * quarter + k for high in (2, 3, 1, 0) for k in low] if quarter else range(count - 1, -1, -1)
 
 
-STEP = 8
+STEP = 16
 
 
 def body(wave_parts, level_table, phase_angles):

time: 67.6 us -> 67.2 us (level); the launches traced: 67.4 us -> 66.2 us
  Pallas kernels: 65.1 us -> 63.9 us
    pallas_call x1, Pallas kernels: 65.1 us -> 63.9 us  [body(): pl.pallas_call(functools.partial(kernel, na, nb, scales), out_shape=jax.S...]
where the time goes in v4:
time: 67.2 us; the launch traced here: 66.2 us
  Pallas kernels  63.9 us (95%)
  local copies, waits for them, and re-layouts  2.3 us (3%)
    pallas_call x1, Pallas kernels, body(): pl.pallas_call(functools.partial(kernel, na, nb, scales), out_shape=jax.S...  63.9 us
    unnamed x1, local copies, waits for them, and re-layouts  2.3 us

profile of v4, /device:TPU:0, one launch (start us, length us, event | category | flops | bytes accessed | tf_op | source)
XLA Modules:
  0.0 66.2 jit_solution(11659983474561218905)
XLA Ops:
  0.0 63.9 %shard_map.37 = f32[2,32,32,128]{3,2,1,0:T(8,128)} custom-call(f32[2,32,32,128]{3,2,1,0:T(8,128)} %bitcast.4, f32[32,32,128]{2,1,0:T(8,128)} %bitcast.5, f32[2,128]{1,0:T(2,128)} %angle_hbm.1), custom_call_target="tpu_custom_call" | custom-call | tf_op jit(solution)/shard_map/pallas_call | solution.py:230
  63.9 2.3 %copy.5 = f32[2,8,128,128]{3,2,1,0:T(8,128)} copy(f32[2,8,128,128]{3,2,1,0:T(8,128)} %bitcast.3) | data formatting | bytes 2097152
